TPU v7x, 128 devices: a whole 4x4x4 slice. The times are simulated.
128 devices in a mesh: gx: 4 (over z_lo, core), gy: 4 (over y), gz: 8 (over x, z_hi).
Axes of the slice: x: 4, y: 4, z: 4 (z_hi: 2, z_lo: 2; z = z_hi * 2 + z_lo), core: 2. Of those that a mesh axis runs over, the one named last changes fastest.
Arguments:
- gradients: bfloat16 [128, 3072, 512], P(('gx', 'gy', 'gz')), may hold values from -24 to 24
- master_weights: float32 [3072, 512], P(('gx', 'gy', 'gz')), may hold values from -10 to 10
- first_moment: float32 [3072, 512], P(('gx', 'gy', 'gz')), may hold values from -8 to 8
- second_moment: float32 [3072, 512], P(('gx', 'gy', 'gz')), may hold values from 1 to 100
- tensor_ids: int32 [3072], P(('gx', 'gy', 'gz')), may hold values from 0 to 3, as said below
Outputs:
- new_master: float32 [3072, 512], P(('gx', 'gy', 'gz'))
- new_first: float32 [3072, 512], P(('gx', 'gy', 'gz'))
- new_second: float32 [3072, 512], P(('gx', 'gy', 'gz'))
- scaled_update: float32 [3072, 512], P(('gx', 'gy', 'gz'))
- params: bfloat16 [3072, 512], replicated
Inputs may be any that keep to these rules, and one draw needn't show every extreme that they name: `tensor_ids`: nondecreasing along the rows; every tensor of 4 owns one contiguous run of rows.
All inputs are finite; a program needn't handle non-finite values.
Results may differ from a plain program's by a relative error of at most 0.0045.
Values may be sent and summed in bfloat16 or wider, within the bound.
No kernel may reach another device: no remote copies, remote signals or barrier semaphores. Data moves between devices by JAX's collectives and lax.ppermute only.
A program may use at most 64 MiB of HBM per device.

v0:
```python
import functools
import jax
import jax.numpy as jnp
from jax import lax
from jax.sharding import Mesh
from jax.sharding import PartitionSpec as P

NT = 4
GX = ("gx_0", "gx_1")
GZ = ("gz_0", "gz_1")
GX_GY_GZ = ("gx_0", "gx_1", "gy", "gz_0", "gz_1")
decay_first = 0.9
decay_second = 0.999
epsilon = 1e-06
weight_decay = 0.01
step_size = 0.05


def split_up(value, dim, length):
    before, after = (value.shape[:dim], value.shape[dim + 1 :])
    return jnp.moveaxis(value.reshape(*before, length, -1, *after), dim, 0)


def sum_at_owner(value, axis, dim):
    blocks = split_up(value, dim, lax.axis_size(axis))
    arrived = lax.all_to_all(blocks, axis, split_axis=0, concat_axis=0, tiled=True)
    return arrived.astype(jnp.float32).sum(axis=0)


def one_axis_at_a_time(value, axes):
    return functools.reduce(lax.psum, axes, value)


def copy_for_each(value, axis):
    length = lax.axis_size(axis)
    return lax.all_to_all(
        jnp.broadcast_to(value[None], (length, *value.shape)), axis, 0, 0, tiled=True
    )


def laid_out(blocks, dim):
    lengths = list(blocks.shape[1:])
    lengths[dim] *= blocks.shape[0]
    return jnp.moveaxis(blocks, 0, dim).reshape(lengths)


def gather_directly(value, axis, dim):
    blocks = copy_for_each(value, axis)
    return laid_out(blocks, dim)


def tensor_sums(values, onehot):
    return jnp.dot(jnp.sum(values * values, axis=1), onehot, precision=lax.Precision.HIGHEST)


def on_device(gradients, master_weights, first_moment, second_moment, tensor_ids):
    count_across = lax.axis_size(GX)
    count_down = lax.axis_size("gy")
    count_along = lax.axis_size(GZ)
    own_rows, row_width = master_weights.shape
    own_gradient = gradients[0].astype(jnp.float32)
    onehot = (tensor_ids[:, None] == jnp.arange(NT, dtype=jnp.int32)[None, :]).astype(jnp.float32)
    counts = jnp.sum(onehot, axis=0) * row_width
    weight_local = tensor_sums(master_weights, onehot)
    blocks = own_gradient.reshape(count_across, count_down, count_along, own_rows, row_width)
    third_rows = own_rows // 3
    first_part = blocks[:, :, :, :third_rows]
    first_part = sum_at_owner(first_part.astype(jnp.bfloat16), GX, 0)
    first_part = sum_at_owner(first_part.astype(jnp.bfloat16), "gy", 1)
    first_part = sum_at_owner(first_part.astype(jnp.bfloat16), GZ, 2)
    second_part = blocks[:, :, :, third_rows : 2 * third_rows]
    second_part = sum_at_owner(second_part.astype(jnp.bfloat16), "gy", 1)
    second_part = sum_at_owner(second_part.astype(jnp.bfloat16), GZ, 2)
    second_part = sum_at_owner(second_part.astype(jnp.bfloat16), GX, 0)
    third_part = blocks[:, :, :, 2 * third_rows :]
    third_part = sum_at_owner(third_part.astype(jnp.bfloat16), GZ, 2)
    third_part = sum_at_owner(third_part.astype(jnp.bfloat16), GX, 0)
    third_part = sum_at_owner(third_part.astype(jnp.bfloat16), "gy", 1)
    summed = jnp.concatenate((first_part, second_part, third_part), axis=3).reshape(
        own_rows, row_width
    )
    new_first = decay_first * first_moment + (1.0 - decay_first) * summed
    new_second = decay_second * second_moment + (1.0 - decay_second) * summed * summed
    update = new_first / (jnp.sqrt(new_second) + epsilon) + weight_decay * master_weights
    update_local = tensor_sums(update, onehot)
    weight_sq, update_sq, total_counts = (
        one_axis_at_a_time(weight_local, GX_GY_GZ),
        one_axis_at_a_time(update_local, GX_GY_GZ),
        one_axis_at_a_time(counts, GX_GY_GZ),
    )
    trust_ratio = jnp.sqrt(weight_sq / (update_sq + total_counts))
    row_trust = jnp.dot(onehot, trust_ratio, precision=lax.Precision.HIGHEST)
    scaled_update = row_trust[:, None] * update
    new_master = master_weights - step_size * scaled_update
    params = new_master.astype(jnp.bfloat16)
    stacked = params.reshape(1, 1, 1, own_rows, row_width)
    stacked = gather_directly(stacked, GZ, 2)
    stacked = gather_directly(stacked, "gy", 1)
    stacked = lax.all_gather(stacked, GX, axis=0, tiled=True)
    gathered = stacked.reshape(count_across * count_down * count_along * own_rows, row_width)
    return (new_master, new_first, new_second, scaled_update, gathered)


def solution(mesh):
    torus = Mesh(
        mesh.devices.reshape(2, 2, mesh.shape["gy"], 4, 2), ("gx_0", "gx_1", "gy", "gz_0", "gz_1")
    )
    return jax.shard_map(
        on_device,
        mesh=torus,
        in_specs=(
            P(GX_GY_GZ, None, None),
            P(GX_GY_GZ, None),
            P(GX_GY_GZ, None),
            P(GX_GY_GZ, None),
            P(GX_GY_GZ),
        ),
        out_specs=(P(GX_GY_GZ, None), P(GX_GY_GZ, None), P(GX_GY_GZ, None), P(GX_GY_GZ, None), P()),
        check_vma=False,
    )
```

profile of v0, /device:TPU:1, one launch (start us, length us, event | category | flops | bytes accessed | tf_op | source)
XLA Modules:
  0.0 229.2 jit_solution(9659133965096885783)
XLA Ops:
  10.3 4.9 %all-to-all-start = ((bf16[4,1,4,8,8,512]{5,4,3,2,1,0:T(8,128)(2,1)}), bf16[4,1,4,8,8,512]{5,4,3,2,1,0:T(8,128)(2,1)S(1)}, u32[]{:S(2)}, u32[]{:S(2)}) async-start(bf16[4,1,4,8,8,512]{5,4,3,2,1,0:T(8,128)(2,1)} %get-tuple-element.22), calls=%async_computation | async-start | bytes 2097152 | tf_op jit(solution)/shard_map/all_to_all | solution.py:26
  16.2 12.4 %all-to-all-done = bf16[4,1,4,8,8,512]{5,4,3,2,1,0:T(8,128)(2,1)S(1)} async-done(((bf16[4,1,4,8,8,512]{5,4,3,2,1,0:T(8,128)(2,1)}), bf16[4,1,4,8,8,512]{5,4,3,2,1,0:T(8,128)(2,1)S(1)}, u32[]{:S(2)}, u32[]{:S(2)}) %all-to-all-start) | async-done | bytes 1048608 | tf_op jit(solution)/shard_map/all_to_all | solution.py:26
  28.6 4.3 %all-to-all-start.3 = ((bf16[4,4,1,8,8,512]{5,4,3,1,2,0:T(8,128)(2,1)}), bf16[4,4,1,8,8,512]{5,4,3,1,2,0:T(8,128)(2,1)S(1)}, u32[]{:S(2)}, u32[]{:S(2)}) async-start(bf16[4,4,1,8,8,512]{5,4,3,1,2,0:T(8,128)(2,1)} %copy.15), calls=%async_computation.3 | async-start | bytes 2097152 | tf_op jit(solution)/shard_map/all_to_all | solution.py:26
  34.0 12.8 %all-to-all-done.3 = bf16[4,4,1,8,8,512]{5,4,3,1,2,0:T(8,128)(2,1)S(1)} async-done(((bf16[4,4,1,8,8,512]{5,4,3,1,2,0:T(8,128)(2,1)}), bf16[4,4,1,8,8,512]{5,4,3,1,2,0:T(8,128)(2,1)S(1)}, u32[]{:S(2)}, u32[]{:S(2)}) %all-to-all-start.3) | async-done | bytes 1048608 | tf_op jit(solution)/shard_map/all_to_all | solution.py:26
  46.9 7.3 %all-to-all-start.6 = ((bf16[8,4,4,1,8,512]{5,4,2,1,3,0:T(8,128)(2,1)}), bf16[8,4,4,1,8,512]{5,4,2,1,3,0:T(8,128)(2,1)S(1)}, u32[]{:S(2)}, u32[]{:S(2)}) async-start(bf16[8,4,4,1,8,512]{5,4,2,1,3,0:T(8,128)(2,1)} %copy.17), calls=%async_computation.6 | async-start | bytes 2097152 | tf_op jit(solution)/shard_map/all_to_all | solution.py:26
  55.1 13.5 %all-to-all-done.6 = bf16[8,4,4,1,8,512]{5,4,2,1,3,0:T(8,128)(2,1)S(1)} async-done(((bf16[8,4,4,1,8,512]{5,4,2,1,3,0:T(8,128)(2,1)}), bf16[8,4,4,1,8,512]{5,4,2,1,3,0:T(8,128)(2,1)S(1)}, u32[]{:S(2)}, u32[]{:S(2)}) %all-to-all-start.6) | async-done | bytes 1048608 | tf_op jit(solution)/shard_map/all_to_all | solution.py:26
  68.6 3.4 %all-to-all-start.1 = ((bf16[4,1,1,8,8,512]{5,4,3,2,1,0:T(8,128)(2,1)}), bf16[4,1,1,8,8,512]{5,4,3,2,1,0:T(8,128)(2,1)S(1)}, u32[]{:S(2)}, u32[]{:S(2)}) async-start(bf16[4,1,1,8,8,512]{5,4,3,2,1,0:T(8,128)(2,1)} %bitcast.4), calls=%async_computation.1 | async-start | bytes 524288 | tf_op jit(solution)/shard_map/all_to_all | solution.py:26
  72.9 4.7 %all-to-all-done.1 = bf16[4,1,1,8,8,512]{5,4,3,2,1,0:T(8,128)(2,1)S(1)} async-done(((bf16[4,1,1,8,8,512]{5,4,3,2,1,0:T(8,128)(2,1)}), bf16[4,1,1,8,8,512]{5,4,3,2,1,0:T(8,128)(2,1)S(1)}, u32[]{:S(2)}, u32[]{:S(2)}) %all-to-all-start.1) | async-done | bytes 262176 | tf_op jit(solution)/shard_map/all_to_all | solution.py:26
  77.5 7.2 %all-to-all-start.7 = ((bf16[4,1,4,1,8,512]{5,4,2,3,1,0:T(8,128)(2,1)}), bf16[4,1,4,1,8,512]{5,4,2,3,1,0:T(8,128)(2,1)S(1)}, u32[]{:S(2)}, u32[]{:S(2)}) async-start(bf16[4,1,4,1,8,512]{5,4,2,3,1,0:T(8,128)(2,1)} %bitcast.15), calls=%async_computation.7 | async-start | bytes 262144 | tf_op jit(solution)/shard_map/all_to_all | solution.py:26
  88.3 3.5 %all-to-all-start.4 = ((bf16[8,4,1,1,8,512]{5,4,1,3,2,0:T(8,128)(2,1)}), bf16[8,4,1,1,8,512]{5,4,1,3,2,0:T(8,128)(2,1)S(1)}, u32[]{:S(2)}, u32[]{:S(2)}) async-start(bf16[8,4,1,1,8,512]{5,4,1,3,2,0:T(8,128)(2,1)} %copy.16), calls=%async_computation.4 | async-start | bytes 524288 | tf_op jit(solution)/shard_map/all_to_all | solution.py:26
  92.5 6.6 %all-to-all-done.4 = bf16[8,4,1,1,8,512]{5,4,1,3,2,0:T(8,128)(2,1)S(1)} async-done(((bf16[8,4,1,1,8,512]{5,4,1,3,2,0:T(8,128)(2,1)}), bf16[8,4,1,1,8,512]{5,4,1,3,2,0:T(8,128)(2,1)S(1)}, u32[]{:S(2)}, u32[]{:S(2)}) %all-to-all-start.4) | async-done | bytes 262176 | tf_op jit(solution)/shard_map/all_to_all | solution.py:26
  99.1 3.3 %all-to-all-start.2 = ((bf16[8,1,1,1,8,512]{5,4,3,2,1,0:T(8,128)(2,1)}), bf16[8,1,1,1,8,512]{5,4,3,2,1,0:T(8,128)(2,1)S(1)}, u32[]{:S(2)}, u32[]{:S(2)}) async-start(bf16[8,1,1,1,8,512]{5,4,3,2,1,0:T(8,128)(2,1)} %bitcast.5), calls=%async_computation.2 | async-start | bytes 131072 | tf_op jit(solution)/shard_map/all_to_all | solution.py:26
  103.9 5.1 %all-to-all-done.2 = bf16[8,1,1,1,8,512]{5,4,3,2,1,0:T(8,128)(2,1)S(1)} async-done(((bf16[8,1,1,1,8,512]{5,4,3,2,1,0:T(8,128)(2,1)}), bf16[8,1,1,1,8,512]{5,4,3,2,1,0:T(8,128)(2,1)S(1)}, u32[]{:S(2)}, u32[]{:S(2)}) %all-to-all-start.2) | async-done | bytes 65568 | tf_op jit(solution)/shard_map/all_to_all | solution.py:26
  112.3 4.2 %all-to-all-done.8 = bf16[4,1,1,1,8,512]{5,4,3,2,1,0:T(8,128)(2,1)S(1)} async-done(((bf16[4,1,1,1,8,512]{5,4,3,2,1,0:T(8,128)(2,1)}), bf16[4,1,1,1,8,512]{5,4,3,2,1,0:T(8,128)(2,1)S(1)}, u32[]{:S(2)}, u32[]{:S(2)}) %all-to-all-start.8) | async-done | bytes 32800 | tf_op jit(solution)/shard_map/all_to_all | solution.py:26
  116.6 8.0 %all-to-all-start.5 = ((bf16[4,1,1,1,8,512]{5,4,3,2,1,0:T(8,128)(2,1)}), bf16[4,1,1,1,8,512]{5,4,3,2,1,0:T(8,128)(2,1)S(1)}, u32[]{:S(2)}, u32[]{:S(2)}) async-start(bf16[4,1,1,1,8,512]{5,4,3,2,1,0:T(8,128)(2,1)} %bitcast.11), calls=%async_computation.5 | async-start | bytes 65536 | tf_op jit(solution)/shard_map/all_to_all | solution.py:26
  128.8 3.8 %all-reduce.4 = (f32[4]{0:T(128)S(1)}, f32[4]{0:T(128)S(1)}) all-reduce(f32[4]{0:T(128)S(1)} %convolution_bitcast_fusion.2, f32[4]{0:T(128)S(1)} %fusion), channel_id=1, replica_groups=mesh['gx_0'=2,'gx_1'=2,'gy'=4,'gz_0'=4,'gz_1'=2] {'gx_0'}, use_global_device_ids=true, to_apply=%region_1.0 | all-reduce | flops 8 | bytes 64 | tf_op jit(solution)/shard_map/psum | solution.py:31
  132.6 4.0 %all-reduce.3 = (f32[4]{0:T(128)S(1)}, f32[4]{0:T(128)S(1)}) all-reduce(f32[4]{0:T(128)S(1)} %get-tuple-element.13, f32[4]{0:T(128)S(1)} %get-tuple-element.14), channel_id=1, replica_groups=mesh['gx_0'=2,'gx_1'=2,'gy'=4,'gz_0'=4,'gz_1'=2] {'gx_1'}, use_global_device_ids=true, to_apply=%region_2.0 | all-reduce | flops 8 | bytes 64 | tf_op jit(solution)/shard_map/psum | solution.py:31
  136.6 6.8 %all-reduce.1 = (f32[4]{0:T(128)S(1)}, f32[4]{0:T(128)S(1)}) all-reduce(f32[4]{0:T(128)S(1)} %get-tuple-element.11, f32[4]{0:T(128)S(1)} %get-tuple-element.12), channel_id=1, replica_groups=mesh['gx_0'=2,'gx_1'=2,'gy'=4,'gz_0'=4,'gz_1'=2] {'gy'}, use_global_device_ids=true, to_apply=%region_3.0 | all-reduce | flops 8 | bytes 64 | tf_op jit(solution)/shard_map/psum | solution.py:31
  143.4 6.9 %all-reduce = (f32[4]{0:T(128)S(1)}, f32[4]{0:T(128)S(1)}) all-reduce(f32[4]{0:T(128)S(1)} %get-tuple-element.7, f32[4]{0:T(128)S(1)} %get-tuple-element.8), channel_id=1, replica_groups=mesh['gx_0'=2,'gx_1'=2,'gy'=4,'gz_0'=4,'gz_1'=2] {'gz_0'}, use_global_device_ids=true, to_apply=%region_4.0 | all-reduce | flops 8 | bytes 64 | tf_op jit(solution)/shard_map/psum | solution.py:31
  150.3 5.3 %all-reduce.2 = (f32[4]{0:T(128)S(1)}, f32[4]{0:T(128)S(1)}) all-reduce(f32[4]{0:T(128)S(1)} %get-tuple-element.5, f32[4]{0:T(128)S(1)} %get-tuple-element.6), channel_id=1, replica_groups=mesh['gx_0'=2,'gx_1'=2,'gy'=4,'gz_0'=4,'gz_1'=2] {'gz_1'}, use_global_device_ids=true, to_apply=%region_5.0 | all-reduce | flops 8 | bytes 64 | tf_op jit(solution)/shard_map/psum | solution.py:31
  156.4 9.4 %all_to_all.55 = bf16[8,1,1,1,24,512]{5,4,3,2,1,0:T(8,128)(2,1)S(1)} all-to-all(bf16[8,1,1,1,24,512]{5,4,3,2,1,0:T(8,128)(2,1)S(1)} %broadcast_in_dim.6), channel_id=1, replica_groups=mesh['gx_0'=2,'gx_1'=2,'gy'=4,'gz_0'=4,'gz_1'=2] {'gz_0','gz_1'}, dimensions={0} | all-to-all | bytes 393216 | tf_op jit(solution)/shard_map/all_to_all | solution.py:36
  165.9 11.5 %all_to_all.56 = bf16[4,1,1,8,24,512]{5,4,3,2,1,0:T(8,128)(2,1)} all-to-all(bf16[4,1,1,8,24,512]{5,4,3,2,1,0:T(8,128)(2,1)S(1)} %broadcast_in_dim.8), channel_id=1, replica_groups=mesh['gx_0'=2,'gx_1'=2,'gy'=4,'gz_0'=4,'gz_1'=2] {'gy'}, dimensions={0} | all-to-all | bytes 1572864 | tf_op jit(solution)/shard_map/all_to_all | solution.py:36
  177.4 41.2 %all-gather.3.cloned.1.call-done = bf16[16,1,1,8,24,512]{5,4,3,2,1,0:T(8,128)(2,1)} async-done(((bf16[4,1,1,8,24,512]{5,4,3,2,1,0:T(8,128)(2,1)}), bf16[16,1,1,8,24,512]{5,4,3,2,1,0:T(8,128)(2,1)}) %all-gather.3.cloned.1.call-update) | async-done | bytes 3145744 | tf_op jit(solution)/shard_map/all_gather | solution.py:99
  218.6 3.8 %copy.19 = bf16[3072,512]{1,0:T(8,128)(2,1)} copy(bf16[3072,512]{1,0:T(8,128)(2,1)} %bitcast.50) | data formatting | bytes 6291456
  (34 shorter events, 21.1 us)
Async XLA Ops:
  10.3 18.3 %all-to-all-start = ((bf16[4,1,4,8,8,512]{5,4,3,2,1,0:T(8,128)(2,1)}), bf16[4,1,4,8,8,512]{5,4,3,2,1,0:T(8,128)(2,1)S(1)}, u32[]{:S(2)}, u32[]{:S(2)}) async-start(bf16[4,1,4,8,8,512]{5,4,3,2,1,0:T(8,128)(2,1)} %get-tuple-element.22), calls=%async_computation | async-start | bytes 2097152 | tf_op jit(solution)/shard_map/all_to_all | solution.py:26
  28.6 18.3 %all-to-all-start.3 = ((bf16[4,4,1,8,8,512]{5,4,3,1,2,0:T(8,128)(2,1)}), bf16[4,4,1,8,8,512]{5,4,3,1,2,0:T(8,128)(2,1)S(1)}, u32[]{:S(2)}, u32[]{:S(2)}) async-start(bf16[4,4,1,8,8,512]{5,4,3,1,2,0:T(8,128)(2,1)} %copy.15), calls=%async_computation.3 | async-start | bytes 2097152 | tf_op jit(solution)/shard_map/all_to_all | solution.py:26
  46.9 21.8 %all-to-all-start.6 = ((bf16[8,4,4,1,8,512]{5,4,2,1,3,0:T(8,128)(2,1)}), bf16[8,4,4,1,8,512]{5,4,2,1,3,0:T(8,128)(2,1)S(1)}, u32[]{:S(2)}, u32[]{:S(2)}) async-start(bf16[8,4,4,1,8,512]{5,4,2,1,3,0:T(8,128)(2,1)} %copy.17), calls=%async_computation.6 | async-start | bytes 2097152 | tf_op jit(solution)/shard_map/all_to_all | solution.py:26
  54.2 48.3 %copy-start.3 = (s32[24]{0:T(128)S(1)}, s32[24]{0:T(128)}, u32[]{:S(2)}) copy-start(s32[24]{0:T(128)} %param.9) | copy-start | bytes 292
  54.2 73.5 %copy-start = (f32[24,512]{1,0:T(8,128)S(1)}, f32[24,512]{1,0:T(8,128)}, u32[]{:S(2)}) copy-start(f32[24,512]{1,0:T(8,128)} %param.6) | copy-start | bytes 147460
  54.2 73.5 %copy-start.1 = (f32[24,512]{1,0:T(8,128)S(1)}, f32[24,512]{1,0:T(8,128)}, u32[]{:S(2)}) copy-start(f32[24,512]{1,0:T(8,128)} %param.8) | copy-start | bytes 147460
  54.2 73.5 %copy-start.2 = (f32[24,512]{1,0:T(8,128)S(1)}, f32[24,512]{1,0:T(8,128)}, u32[]{:S(2)}) copy-start(f32[24,512]{1,0:T(8,128)} %param.7) | copy-start | bytes 147460
  68.6 8.9 %all-to-all-start.1 = ((bf16[4,1,1,8,8,512]{5,4,3,2,1,0:T(8,128)(2,1)}), bf16[4,1,1,8,8,512]{5,4,3,2,1,0:T(8,128)(2,1)S(1)}, u32[]{:S(2)}, u32[]{:S(2)}) async-start(bf16[4,1,1,8,8,512]{5,4,3,2,1,0:T(8,128)(2,1)} %bitcast.4), calls=%async_computation.1 | async-start | bytes 524288 | tf_op jit(solution)/shard_map/all_to_all | solution.py:26
  77.5 10.8 %all-to-all-start.7 = ((bf16[4,1,4,1,8,512]{5,4,2,3,1,0:T(8,128)(2,1)}), bf16[4,1,4,1,8,512]{5,4,2,3,1,0:T(8,128)(2,1)S(1)}, u32[]{:S(2)}, u32[]{:S(2)}) async-start(bf16[4,1,4,1,8,512]{5,4,2,3,1,0:T(8,128)(2,1)} %bitcast.15), calls=%async_computation.7 | async-start | bytes 262144 | tf_op jit(solution)/shard_map/all_to_all | solution.py:26
  88.3 10.8 %all-to-all-start.4 = ((bf16[8,4,1,1,8,512]{5,4,1,3,2,0:T(8,128)(2,1)}), bf16[8,4,1,1,8,512]{5,4,1,3,2,0:T(8,128)(2,1)S(1)}, u32[]{:S(2)}, u32[]{:S(2)}) async-start(bf16[8,4,1,1,8,512]{5,4,1,3,2,0:T(8,128)(2,1)} %copy.16), calls=%async_computation.4 | async-start | bytes 524288 | tf_op jit(solution)/shard_map/all_to_all | solution.py:26
  99.1 9.9 %all-to-all-start.2 = ((bf16[8,1,1,1,8,512]{5,4,3,2,1,0:T(8,128)(2,1)}), bf16[8,1,1,1,8,512]{5,4,3,2,1,0:T(8,128)(2,1)S(1)}, u32[]{:S(2)}, u32[]{:S(2)}) async-start(bf16[8,1,1,1,8,512]{5,4,3,2,1,0:T(8,128)(2,1)} %bitcast.5), calls=%async_computation.2 | async-start | bytes 131072 | tf_op jit(solution)/shard_map/all_to_all | solution.py:26
  109.0 7.5 %all-to-all-start.8 = ((bf16[4,1,1,1,8,512]{5,4,3,2,1,0:T(8,128)(2,1)}), bf16[4,1,1,1,8,512]{5,4,3,2,1,0:T(8,128)(2,1)S(1)}, u32[]{:S(2)}, u32[]{:S(2)}) async-start(bf16[4,1,1,1,8,512]{5,4,3,2,1,0:T(8,128)(2,1)} %bitcast.16), calls=%async_computation.8 | async-start | bytes 65536 | tf_op jit(solution)/shard_map/all_to_all | solution.py:26
  116.6 11.2 %all-to-all-start.5 = ((bf16[4,1,1,1,8,512]{5,4,3,2,1,0:T(8,128)(2,1)}), bf16[4,1,1,1,8,512]{5,4,3,2,1,0:T(8,128)(2,1)S(1)}, u32[]{:S(2)}, u32[]{:S(2)}) async-start(bf16[4,1,1,1,8,512]{5,4,3,2,1,0:T(8,128)(2,1)} %bitcast.11), calls=%async_computation.5 | async-start | bytes 65536 | tf_op jit(solution)/shard_map/all_to_all | solution.py:26
  124.6 94.0 %all-gather.3.cloned.1.call-start = ((), (), s32[]{:S(2)}) async-start(), calls=%async_computation.11 | async-start | bytes 3932160 | tf_op jit(solution)/shard_map/all_gather | solution.py:99
Sparse Core Ops, SparseCore 0:
  177.5 40.9 all-gather.2
where the time goes:
time: 230 us; the launch traced here: 229 us
  waiting for transfers between devices  106 us (46%)
  blocking collectives  47.7 us (21%)
  starting transfers between devices  45.3 us (20%)
  between operations  14.1 us (6%)
  local copies, waits for them, and re-layouts  9.9 us (4%)
  other arithmetic  5.55 us (2%)
    all_to_all x9, waiting for transfers between devices, sum_at_owner(): lax.all_to_all(blocks, axis, split_axis=0, concat_axis=0, tiled=True)  65.1 us
    all_to_all x9, starting transfers between devices, sum_at_owner(): lax.all_to_all(blocks, axis, split_axis=0, concat_axis=0, tiled=True)  45.3 us
    all_gather x1, waiting for transfers between devices, on_device(): stacked = lax.all_gather(stacked, GX, axis=0, tiled=True)  41.2 us
    psum x5, blocking collectives, one_axis_at_a_time(): return functools.reduce(lax.psum, axes, value)  26.8 us
    all_to_all x2, blocking collectives, copy_for_each(): lax.all_to_all(jnp.broadcast_to(value[None], (length, *value.shape)), axi...  20.9 us
  transfers between devices with their start and end apart: 10, of which 10 were waited for; matrix products, arithmetic and copies ran while one was open for 3% of the time, Pallas kernels for 0%

commit v1 on v0

--- a/solution.py
+++ b/solution.py
@@ -96,7 +96,10 @@
     stacked = params.reshape(1, 1, 1, own_rows, row_width)
     stacked = gather_directly(stacked, GZ, 2)
     stacked = gather_directly(stacked, "gy", 1)
-    stacked = lax.all_gather(stacked, GX, axis=0, tiled=True)
+    size = lax.axis_size(GX)
+    parts = jnp.stack([stacked for _ in range(size)])
+    parts = lax.all_to_all(parts, GX, split_axis=0, concat_axis=0)
+    stacked = jnp.concatenate(parts, axis=0)
     gathered = stacked.reshape(count_across * count_down * count_along * own_rows, row_width)
     return (new_master, new_first, new_second, scaled_update, gathered)
 

time: 230 us -> 219 us (0.952)
  blocking collectives: 47.7 us -> 93.2 us
  waiting for transfers between devices: 106 us -> 65.1 us
  between operations: 14.1 us -> 0.77 us
    all_to_all x0 -> x1, blocking collectives: none -> 46.2 us  [on_device(): parts = lax.all_to_all(parts, GX, split_axis=0, concat_axis=0)]
    all_gather x1 -> x0, waiting for transfers between devices: 41.2 us -> none  [on_device(): stacked = lax.all_gather(stacked, GX, axis=0, tiled=True)]
  transfers between devices with their start and end apart: 10 -> 9, of which waited for: 10 -> 9; matrix products, arithmetic and copies ran while one was open for 3% -> 3% of each run, Pallas kernels for 0% -> 0%
where the time goes in v1:
time: 219 us; the launch traced here: 218 us
  blocking collectives  93.2 us (43%)
  waiting for transfers between devices  65.1 us (30%)
  starting transfers between devices  45.3 us (21%)
  local copies, waits for them, and re-layouts  8.12 us (4%)
  other arithmetic  5.55 us (3%)
    all_to_all x9, waiting for transfers between devices, sum_at_owner(): lax.all_to_all(blocks, axis, split_axis=0, concat_axis=0, tiled=True)  65.1 us
    all_to_all x1, blocking collectives, on_device(): parts = lax.all_to_all(parts, GX, split_axis=0, concat_axis=0)  46.2 us
    all_to_all x9, starting transfers between devices, sum_at_owner(): lax.all_to_all(blocks, axis, split_axis=0, concat_axis=0, tiled=True)  45.3 us
    psum x5, blocking collectives, one_axis_at_a_time(): return functools.reduce(lax.psum, axes, value)  26.8 us
    all_to_all x2, blocking collectives, copy_for_each(): lax.all_to_all(jnp.broadcast_to(value[None], (length, *value.shape)), axi...  20.2 us
  transfers between devices with their start and end apart: 9, of which 9 were waited for; matrix products, arithmetic and copies ran while one was open for 3% of the time, Pallas kernels for 0%

profile of v1, /device:TPU:1, one launch (start us, length us, event | category | flops | bytes accessed | tf_op | source)
XLA Modules:
  0.0 218.3 jit_solution(1322613680117789636)
XLA Ops:
  3.8 4.9 %all-to-all-start = ((bf16[4,1,4,8,8,512]{5,4,3,2,1,0:T(8,128)(2,1)}), bf16[4,1,4,8,8,512]{5,4,3,2,1,0:T(8,128)(2,1)S(1)}, u32[]{:S(2)}, u32[]{:S(2)}) async-start(bf16[4,1,4,8,8,512]{5,4,3,2,1,0:T(8,128)(2,1)} %get-tuple-element.22), calls=%async_computation | async-start | bytes 2097152 | tf_op jit(solution)/shard_map/all_to_all | solution.py:26
  9.7 12.4 %all-to-all-done = bf16[4,1,4,8,8,512]{5,4,3,2,1,0:T(8,128)(2,1)S(1)} async-done(((bf16[4,1,4,8,8,512]{5,4,3,2,1,0:T(8,128)(2,1)}), bf16[4,1,4,8,8,512]{5,4,3,2,1,0:T(8,128)(2,1)S(1)}, u32[]{:S(2)}, u32[]{:S(2)}) %all-to-all-start) | async-done | bytes 1048608 | tf_op jit(solution)/shard_map/all_to_all | solution.py:26
  22.1 4.3 %all-to-all-start.3 = ((bf16[4,4,1,8,8,512]{5,4,3,1,2,0:T(8,128)(2,1)}), bf16[4,4,1,8,8,512]{5,4,3,1,2,0:T(8,128)(2,1)S(1)}, u32[]{:S(2)}, u32[]{:S(2)}) async-start(bf16[4,4,1,8,8,512]{5,4,3,1,2,0:T(8,128)(2,1)} %copy.15), calls=%async_computation.3 | async-start | bytes 2097152 | tf_op jit(solution)/shard_map/all_to_all | solution.py:26
  27.5 12.8 %all-to-all-done.3 = bf16[4,4,1,8,8,512]{5,4,3,1,2,0:T(8,128)(2,1)S(1)} async-done(((bf16[4,4,1,8,8,512]{5,4,3,1,2,0:T(8,128)(2,1)}), bf16[4,4,1,8,8,512]{5,4,3,1,2,0:T(8,128)(2,1)S(1)}, u32[]{:S(2)}, u32[]{:S(2)}) %all-to-all-start.3) | async-done | bytes 1048608 | tf_op jit(solution)/shard_map/all_to_all | solution.py:26
  40.3 7.3 %all-to-all-start.6 = ((bf16[8,4,4,1,8,512]{5,4,2,1,3,0:T(8,128)(2,1)}), bf16[8,4,4,1,8,512]{5,4,2,1,3,0:T(8,128)(2,1)S(1)}, u32[]{:S(2)}, u32[]{:S(2)}) async-start(bf16[8,4,4,1,8,512]{5,4,2,1,3,0:T(8,128)(2,1)} %copy.17), calls=%async_computation.6 | async-start | bytes 2097152 | tf_op jit(solution)/shard_map/all_to_all | solution.py:26
  48.6 13.5 %all-to-all-done.6 = bf16[8,4,4,1,8,512]{5,4,2,1,3,0:T(8,128)(2,1)S(1)} async-done(((bf16[8,4,4,1,8,512]{5,4,2,1,3,0:T(8,128)(2,1)}), bf16[8,4,4,1,8,512]{5,4,2,1,3,0:T(8,128)(2,1)S(1)}, u32[]{:S(2)}, u32[]{:S(2)}) %all-to-all-start.6) | async-done | bytes 1048608 | tf_op jit(solution)/shard_map/all_to_all | solution.py:26
  62.1 3.4 %all-to-all-start.1 = ((bf16[4,1,1,8,8,512]{5,4,3,2,1,0:T(8,128)(2,1)}), bf16[4,1,1,8,8,512]{5,4,3,2,1,0:T(8,128)(2,1)S(1)}, u32[]{:S(2)}, u32[]{:S(2)}) async-start(bf16[4,1,1,8,8,512]{5,4,3,2,1,0:T(8,128)(2,1)} %bitcast.4), calls=%async_computation.1 | async-start | bytes 524288 | tf_op jit(solution)/shard_map/all_to_all | solution.py:26
  66.3 4.7 %all-to-all-done.1 = bf16[4,1,1,8,8,512]{5,4,3,2,1,0:T(8,128)(2,1)S(1)} async-done(((bf16[4,1,1,8,8,512]{5,4,3,2,1,0:T(8,128)(2,1)}), bf16[4,1,1,8,8,512]{5,4,3,2,1,0:T(8,128)(2,1)S(1)}, u32[]{:S(2)}, u32[]{:S(2)}) %all-to-all-start.1) | async-done | bytes 262176 | tf_op jit(solution)/shard_map/all_to_all | solution.py:26
  71.0 7.2 %all-to-all-start.7 = ((bf16[4,1,4,1,8,512]{5,4,2,3,1,0:T(8,128)(2,1)}), bf16[4,1,4,1,8,512]{5,4,2,3,1,0:T(8,128)(2,1)S(1)}, u32[]{:S(2)}, u32[]{:S(2)}) async-start(bf16[4,1,4,1,8,512]{5,4,2,3,1,0:T(8,128)(2,1)} %bitcast.15), calls=%async_computation.7 | async-start | bytes 262144 | tf_op jit(solution)/shard_map/all_to_all | solution.py:26
  81.8 3.5 %all-to-all-start.4 = ((bf16[8,4,1,1,8,512]{5,4,1,3,2,0:T(8,128)(2,1)}), bf16[8,4,1,1,8,512]{5,4,1,3,2,0:T(8,128)(2,1)S(1)}, u32[]{:S(2)}, u32[]{:S(2)}) async-start(bf16[8,4,1,1,8,512]{5,4,1,3,2,0:T(8,128)(2,1)} %copy.16), calls=%async_computation.4 | async-start | bytes 524288 | tf_op jit(solution)/shard_map/all_to_all | solution.py:26
  86.0 6.6 %all-to-all-done.4 = bf16[8,4,1,1,8,512]{5,4,1,3,2,0:T(8,128)(2,1)S(1)} async-done(((bf16[8,4,1,1,8,512]{5,4,1,3,2,0:T(8,128)(2,1)}), bf16[8,4,1,1,8,512]{5,4,1,3,2,0:T(8,128)(2,1)S(1)}, u32[]{:S(2)}, u32[]{:S(2)}) %all-to-all-start.4) | async-done | bytes 262176 | tf_op jit(solution)/shard_map/all_to_all | solution.py:26
  92.6 3.3 %all-to-all-start.2 = ((bf16[8,1,1,1,8,512]{5,4,3,2,1,0:T(8,128)(2,1)}), bf16[8,1,1,1,8,512]{5,4,3,2,1,0:T(8,128)(2,1)S(1)}, u32[]{:S(2)}, u32[]{:S(2)}) async-start(bf16[8,1,1,1,8,512]{5,4,3,2,1,0:T(8,128)(2,1)} %bitcast.5), calls=%async_computation.2 | async-start | bytes 131072 | tf_op jit(solution)/shard_map/all_to_all | solution.py:26
  97.4 5.1 %all-to-all-done.2 = bf16[8,1,1,1,8,512]{5,4,3,2,1,0:T(8,128)(2,1)S(1)} async-done(((bf16[8,1,1,1,8,512]{5,4,3,2,1,0:T(8,128)(2,1)}), bf16[8,1,1,1,8,512]{5,4,3,2,1,0:T(8,128)(2,1)S(1)}, u32[]{:S(2)}, u32[]{:S(2)}) %all-to-all-start.2) | async-done | bytes 65568 | tf_op jit(solution)/shard_map/all_to_all | solution.py:26
  102.5 3.3 %all-to-all-start.8 = ((bf16[4,1,1,1,8,512]{5,4,3,2,1,0:T(8,128)(2,1)}), bf16[4,1,1,1,8,512]{5,4,3,2,1,0:T(8,128)(2,1)S(1)}, u32[]{:S(2)}, u32[]{:S(2)}) async-start(bf16[4,1,1,1,8,512]{5,4,3,2,1,0:T(8,128)(2,1)} %bitcast.16), calls=%async_computation.8 | async-start | bytes 65536 | tf_op jit(solution)/shard_map/all_to_all | solution.py:26
  105.8 4.2 %all-to-all-done.8 = bf16[4,1,1,1,8,512]{5,4,3,2,1,0:T(8,128)(2,1)S(1)} async-done(((bf16[4,1,1,1,8,512]{5,4,3,2,1,0:T(8,128)(2,1)}), bf16[4,1,1,1,8,512]{5,4,3,2,1,0:T(8,128)(2,1)S(1)}, u32[]{:S(2)}, u32[]{:S(2)}) %all-to-all-start.8) | async-done | bytes 32800 | tf_op jit(solution)/shard_map/all_to_all | solution.py:26
  110.0 8.0 %all-to-all-start.5 = ((bf16[4,1,1,1,8,512]{5,4,3,2,1,0:T(8,128)(2,1)}), bf16[4,1,1,1,8,512]{5,4,3,2,1,0:T(8,128)(2,1)S(1)}, u32[]{:S(2)}, u32[]{:S(2)}) async-start(bf16[4,1,1,1,8,512]{5,4,3,2,1,0:T(8,128)(2,1)} %bitcast.11), calls=%async_computation.5 | async-start | bytes 65536 | tf_op jit(solution)/shard_map/all_to_all | solution.py:26
  122.3 3.8 %all-reduce.4 = (f32[4]{0:T(128)S(1)}, f32[4]{0:T(128)S(1)}) all-reduce(f32[4]{0:T(128)S(1)} %convolution_bitcast_fusion.2, f32[4]{0:T(128)S(1)} %fusion), channel_id=1, replica_groups=mesh['gx_0'=2,'gx_1'=2,'gy'=4,'gz_0'=4,'gz_1'=2] {'gx_0'}, use_global_device_ids=true, to_apply=%region_1.0 | all-reduce | flops 8 | bytes 64 | tf_op jit(solution)/shard_map/psum | solution.py:31
  126.0 4.0 %all-reduce.3 = (f32[4]{0:T(128)S(1)}, f32[4]{0:T(128)S(1)}) all-reduce(f32[4]{0:T(128)S(1)} %get-tuple-element.13, f32[4]{0:T(128)S(1)} %get-tuple-element.14), channel_id=1, replica_groups=mesh['gx_0'=2,'gx_1'=2,'gy'=4,'gz_0'=4,'gz_1'=2] {'gx_1'}, use_global_device_ids=true, to_apply=%region_2.0 | all-reduce | flops 8 | bytes 64 | tf_op jit(solution)/shard_map/psum | solution.py:31
  130.1 6.8 %all-reduce.1 = (f32[4]{0:T(128)S(1)}, f32[4]{0:T(128)S(1)}) all-reduce(f32[4]{0:T(128)S(1)} %get-tuple-element.11, f32[4]{0:T(128)S(1)} %get-tuple-element.12), channel_id=1, replica_groups=mesh['gx_0'=2,'gx_1'=2,'gy'=4,'gz_0'=4,'gz_1'=2] {'gy'}, use_global_device_ids=true, to_apply=%region_3.0 | all-reduce | flops 8 | bytes 64 | tf_op jit(solution)/shard_map/psum | solution.py:31
  136.9 6.9 %all-reduce = (f32[4]{0:T(128)S(1)}, f32[4]{0:T(128)S(1)}) all-reduce(f32[4]{0:T(128)S(1)} %get-tuple-element.7, f32[4]{0:T(128)S(1)} %get-tuple-element.8), channel_id=1, replica_groups=mesh['gx_0'=2,'gx_1'=2,'gy'=4,'gz_0'=4,'gz_1'=2] {'gz_0'}, use_global_device_ids=true, to_apply=%region_4.0 | all-reduce | flops 8 | bytes 64 | tf_op jit(solution)/shard_map/psum | solution.py:31
  143.8 5.3 %all-reduce.2 = (f32[4]{0:T(128)S(1)}, f32[4]{0:T(128)S(1)}) all-reduce(f32[4]{0:T(128)S(1)} %get-tuple-element.5, f32[4]{0:T(128)S(1)} %get-tuple-element.6), channel_id=1, replica_groups=mesh['gx_0'=2,'gx_1'=2,'gy'=4,'gz_0'=4,'gz_1'=2] {'gz_1'}, use_global_device_ids=true, to_apply=%region_5.0 | all-reduce | flops 8 | bytes 64 | tf_op jit(solution)/shard_map/psum | solution.py:31
  149.9 9.4 %all_to_all.60 = bf16[8,1,1,1,24,512]{5,4,3,2,1,0:T(8,128)(2,1)S(1)} all-to-all(bf16[8,1,1,1,24,512]{5,4,3,2,1,0:T(8,128)(2,1)S(1)} %broadcast_in_dim.6), channel_id=1, replica_groups=mesh['gx_0'=2,'gx_1'=2,'gy'=4,'gz_0'=4,'gz_1'=2] {'gz_0','gz_1'}, dimensions={0} | all-to-all | bytes 393216 | tf_op jit(solution)/shard_map/all_to_all | solution.py:36
  159.4 10.7 %all_to_all.61 = bf16[4,1,1,8,24,512]{5,4,3,2,1,0:T(8,128)(2,1)S(1)} all-to-all(bf16[4,1,1,8,24,512]{5,4,3,2,1,0:T(8,128)(2,1)S(1)} %broadcast_in_dim.8), channel_id=1, replica_groups=mesh['gx_0'=2,'gx_1'=2,'gy'=4,'gz_0'=4,'gz_1'=2] {'gy'}, dimensions={0} | all-to-all | bytes 1572864 | tf_op jit(solution)/shard_map/all_to_all | solution.py:36
  170.5 46.2 %all_to_all.62 = bf16[4,1,4,8,24,512]{5,4,3,2,1,0:T(8,128)(2,1)S(1)} all-to-all(bf16[4,1,4,8,24,512]{5,4,3,2,1,0:T(8,128)(2,1)S(1)} %stack.3), channel_id=1, replica_groups=mesh['gx_0'=2,'gx_1'=2,'gy'=4,'gz_0'=4,'gz_1'=2] {'gx_0','gx_1'}, dimensions={0} | all-to-all | bytes 6291456 | tf_op jit(solution)/shard_map/all_to_all | solution.py:101
  (33 shorter events, 19.8 us)
Async XLA Ops:
  3.8 18.3 %all-to-all-start = ((bf16[4,1,4,8,8,512]{5,4,3,2,1,0:T(8,128)(2,1)}), bf16[4,1,4,8,8,512]{5,4,3,2,1,0:T(8,128)(2,1)S(1)}, u32[]{:S(2)}, u32[]{:S(2)}) async-start(bf16[4,1,4,8,8,512]{5,4,3,2,1,0:T(8,128)(2,1)} %get-tuple-element.22), calls=%async_computation | async-start | bytes 2097152 | tf_op jit(solution)/shard_map/all_to_all | solution.py:26
  22.1 18.3 %all-to-all-start.3 = ((bf16[4,4,1,8,8,512]{5,4,3,1,2,0:T(8,128)(2,1)}), bf16[4,4,1,8,8,512]{5,4,3,1,2,0:T(8,128)(2,1)S(1)}, u32[]{:S(2)}, u32[]{:S(2)}) async-start(bf16[4,4,1,8,8,512]{5,4,3,1,2,0:T(8,128)(2,1)} %copy.15), calls=%async_computation.3 | async-start | bytes 2097152 | tf_op jit(solution)/shard_map/all_to_all | solution.py:26
  40.3 21.8 %all-to-all-start.6 = ((bf16[8,4,4,1,8,512]{5,4,2,1,3,0:T(8,128)(2,1)}), bf16[8,4,4,1,8,512]{5,4,2,1,3,0:T(8,128)(2,1)S(1)}, u32[]{:S(2)}, u32[]{:S(2)}) async-start(bf16[8,4,4,1,8,512]{5,4,2,1,3,0:T(8,128)(2,1)} %copy.17), calls=%async_computation.6 | async-start | bytes 2097152 | tf_op jit(solution)/shard_map/all_to_all | solution.py:26
  47.7 48.3 %copy-start.3 = (s32[24]{0:T(128)S(1)}, s32[24]{0:T(128)}, u32[]{:S(2)}) copy-start(s32[24]{0:T(128)} %param.9) | copy-start | bytes 292
  47.7 73.5 %copy-start = (f32[24,512]{1,0:T(8,128)S(1)}, f32[24,512]{1,0:T(8,128)}, u32[]{:S(2)}) copy-start(f32[24,512]{1,0:T(8,128)} %param.6) | copy-start | bytes 147460
  47.7 73.5 %copy-start.1 = (f32[24,512]{1,0:T(8,128)S(1)}, f32[24,512]{1,0:T(8,128)}, u32[]{:S(2)}) copy-start(f32[24,512]{1,0:T(8,128)} %param.8) | copy-start | bytes 147460
  47.7 73.5 %copy-start.2 = (f32[24,512]{1,0:T(8,128)S(1)}, f32[24,512]{1,0:T(8,128)}, u32[]{:S(2)}) copy-start(f32[24,512]{1,0:T(8,128)} %param.7) | copy-start | bytes 147460
  62.1 8.9 %all-to-all-start.1 = ((bf16[4,1,1,8,8,512]{5,4,3,2,1,0:T(8,128)(2,1)}), bf16[4,1,1,8,8,512]{5,4,3,2,1,0:T(8,128)(2,1)S(1)}, u32[]{:S(2)}, u32[]{:S(2)}) async-start(bf16[4,1,1,8,8,512]{5,4,3,2,1,0:T(8,128)(2,1)} %bitcast.4), calls=%async_computation.1 | async-start | bytes 524288 | tf_op jit(solution)/shard_map/all_to_all | solution.py:26
  71.0 10.8 %all-to-all-start.7 = ((bf16[4,1,4,1,8,512]{5,4,2,3,1,0:T(8,128)(2,1)}), bf16[4,1,4,1,8,512]{5,4,2,3,1,0:T(8,128)(2,1)S(1)}, u32[]{:S(2)}, u32[]{:S(2)}) async-start(bf16[4,1,4,1,8,512]{5,4,2,3,1,0:T(8,128)(2,1)} %bitcast.15), calls=%async_computation.7 | async-start | bytes 262144 | tf_op jit(solution)/shard_map/all_to_all | solution.py:26
  81.8 10.8 %all-to-all-start.4 = ((bf16[8,4,1,1,8,512]{5,4,1,3,2,0:T(8,128)(2,1)}), bf16[8,4,1,1,8,512]{5,4,1,3,2,0:T(8,128)(2,1)S(1)}, u32[]{:S(2)}, u32[]{:S(2)}) async-start(bf16[8,4,1,1,8,512]{5,4,1,3,2,0:T(8,128)(2,1)} %copy.16), calls=%async_computation.4 | async-start | bytes 524288 | tf_op jit(solution)/shard_map/all_to_all | solution.py:26
  92.6 9.9 %all-to-all-start.2 = ((bf16[8,1,1,1,8,512]{5,4,3,2,1,0:T(8,128)(2,1)}), bf16[8,1,1,1,8,512]{5,4,3,2,1,0:T(8,128)(2,1)S(1)}, u32[]{:S(2)}, u32[]{:S(2)}) async-start(bf16[8,1,1,1,8,512]{5,4,3,2,1,0:T(8,128)(2,1)} %bitcast.5), calls=%async_computation.2 | async-start | bytes 131072 | tf_op jit(solution)/shard_map/all_to_all | solution.py:26
  102.5 7.5 %all-to-all-start.8 = ((bf16[4,1,1,1,8,512]{5,4,3,2,1,0:T(8,128)(2,1)}), bf16[4,1,1,1,8,512]{5,4,3,2,1,0:T(8,128)(2,1)S(1)}, u32[]{:S(2)}, u32[]{:S(2)}) async-start(bf16[4,1,1,1,8,512]{5,4,3,2,1,0:T(8,128)(2,1)} %bitcast.16), calls=%async_computation.8 | async-start | bytes 65536 | tf_op jit(solution)/shard_map/all_to_all | solution.py:26
  110.0 11.2 %all-to-all-start.5 = ((bf16[4,1,1,1,8,512]{5,4,3,2,1,0:T(8,128)(2,1)}), bf16[4,1,1,1,8,512]{5,4,3,2,1,0:T(8,128)(2,1)S(1)}, u32[]{:S(2)}, u32[]{:S(2)}) async-start(bf16[4,1,1,1,8,512]{5,4,3,2,1,0:T(8,128)(2,1)} %bitcast.11), calls=%async_computation.5 | async-start | bytes 65536 | tf_op jit(solution)/shard_map/all_to_all | solution.py:26
